TPU v7x, 256 devices: a whole 4x4x8 slice. The times are simulated.
256 devices in a mesh: gz: 32 (over z, x_hi, core), vert: 8 (over y, x_lo).
Axes of the slice: x: 4 (x_hi: 2, x_lo: 2; x = x_hi * 2 + x_lo), y: 4, z: 8, core: 2. Of those that a mesh axis runs over, the one named last changes fastest.
Arguments:
- volume: float32 [256, 128, 1024], P('gz'), may hold values from -6 to 6
- angle_index: int32 [32], P('vert'), may hold values from 0 to 511
- detector_rows: int32 [128], replicated, may hold values from 0 to 127, each once
- measured: float32 [32, 128, 1024], P('vert', 'gz'), may hold values from -96 to 96
Outputs:
- residual: float32 [32, 128, 1024], P('vert', 'gz')
- gradient: float32 [256, 128, 1024], P('gz', 'vert')
All inputs are finite; a program needn't handle non-finite values.
Results may differ from a plain program's by a relative error of at most 0.0003.
Values sent between devices are 32-bit elements; how exact they have to be, the bound alone decides.
A program may use at most 64 MiB of HBM per device.

v0:
```python
import jax
import jax.numpy as jnp
from jax import lax
from jax.sharding import PartitionSpec as P

ANGLES = 512


def in_blocks(value, dim, peers):
    dims = value.shape
    tiles = value.reshape(*dims[:dim], peers, dims[dim] // peers, *dims[dim + 1 :])
    return jnp.moveaxis(tiles, dim, 0)


def sent_and_summed(value, axis, dim):
    peers = lax.axis_size(axis)
    tiles = lax.all_to_all(in_blocks(value, dim, peers), axis, 0, 0, tiled=True)
    return jnp.sum(tiles, axis=0)


def in_order(tiles, dim):
    dims = list(tiles.shape[1:])
    dims[dim] *= tiles.shape[0]
    return jnp.moveaxis(tiles, 0, dim).reshape(dims)


def sent_to_all(value, axis):
    copies = jnp.broadcast_to(value, (lax.axis_size(axis), *value.shape))
    return lax.all_to_all(copies, axis, split_axis=0, concat_axis=0, tiled=True)


def gather_directly(value, axis, dim):
    return in_order(sent_to_all(value, axis), dim)


def shifts(depth_pos, angle_value):
    slope_num = 2 * angle_value - ANGLES
    product = depth_pos * slope_num
    shift_whole = jnp.floor_divide(product, ANGLES)
    shift_part = (product - shift_whole * ANGLES).astype(jnp.float32) / ANGLES
    slope_value = slope_num.astype(jnp.float32) / ANGLES
    weight = jnp.sqrt(1.0 + slope_value * slope_value)
    return (shift_whole, shift_part, weight)


def backproject(back, angles, depth_pos, margin):
    columns, row_count = (back.shape[2], back.shape[1])
    back_cols = jnp.transpose(back, (0, 2, 1))
    back_pad = jnp.pad(back_cols, ((0, 0), (margin, margin), (0, 0)))

    def add_view(running, view_item):
        plane, angle_value = view_item
        shift_whole, shift_part, weight = shifts(depth_pos, angle_value)

        def add_shifted(offset, fraction):
            window = lax.dynamic_slice_in_dim(plane, offset, columns + 1, 0)
            return (1.0 - fraction) * window[1:, :] + fraction * window[:-1, :]

        contrib = jax.vmap(add_shifted)(margin - shift_whole - 1, shift_part)
        return (running + weight * contrib, None)

    start_sum = jnp.zeros((depth_pos.shape[0], columns, row_count), jnp.float32)
    summed, _ = lax.scan(add_view, start_sum, (back_pad, angles))
    return jnp.transpose(summed, (0, 2, 1))


def per_device(volume, angle_index, detector_rows, measured):
    layers, row_count, columns = volume.shape
    slab_count = lax.axis_size("gz")
    total_depth = layers * slab_count
    margin = total_depth // 2 + 2
    depth_pos = (
        lax.axis_index("gz") * layers + jnp.arange(layers, dtype=jnp.int32) - total_depth // 2
    )
    vol_cols = jnp.transpose(volume, (0, 2, 1))
    padded = jnp.pad(vol_cols, ((0, 0), (margin, margin), (0, 0)))

    def project(angle_value):
        shift_whole, shift_part, weight = shifts(depth_pos, angle_value)

        def project_shifted(plane, offset, fraction):
            window = lax.dynamic_slice_in_dim(plane, offset, columns + 1, 0)
            return (1.0 - fraction) * window[:-1, :] + fraction * window[1:, :]

        contrib = jax.vmap(project_shifted)(padded, margin + shift_whole, shift_part)
        return weight * jnp.sum(contrib, axis=0)

    partial_cols = lax.map(project, angle_index)
    det_cols = jnp.take(partial_cols, detector_rows, axis=2)
    det_order = jnp.transpose(det_cols, (0, 2, 1))
    res_scale = total_depth ** (-0.5)
    own_rows = sent_and_summed(det_order, "gz", 1)
    residual = (own_rows - measured) * res_scale
    full_rows = gather_directly(residual, "gz", 1)
    back = jnp.zeros_like(full_rows).at[:, detector_rows, :].set(full_rows)
    view_scale = (angle_index.shape[0] * lax.axis_size("vert")) ** (-0.5)
    contrib_all = backproject(back, angle_index, depth_pos, margin)
    gradient = sent_and_summed(contrib_all, "vert", 1) * view_scale
    return (residual, gradient)


def solution(mesh):
    in_specs = (P("gz", None, None), P("vert"), P(), P("vert", "gz", None))
    out_specs = (P("vert", "gz", None), P("gz", "vert", None))
    return jax.shard_map(
        per_device, mesh=mesh, in_specs=in_specs, out_specs=out_specs, check_vma=False
    )
```

profile of v0, /device:TPU:1, one launch (start us, length us, event | category | flops | bytes accessed | tf_op | source)
XLA Modules:
  0.0 513.9 jit_solution(4433344700342288015)
XLA Ops:
  2.0 5.4 %copy.14 = f32[8,128,1024]{1,2,0:T(8,128)} copy(f32[8,128,1024]{2,1,0:T(8,128)} %param.8) | data formatting | bytes 8388608 | tf_op args[0]
  7.3 4.8 pad.20
  12.2 189.6 %while.36 = (s32[]{:T(128)}, f32[4,1024,128]{1,0,2:T(4,128)}, s32[4]{0:T(128)S(1)}, f32[8,1284,128]{2,1,0:T(8,128)}, s32[]{:T(128)}, /*index=5*/s32[]{:T(128)}, ...) while((s32[]{:T(128)}, f32[4,1024,128]{1,0,2:T(4,128)}, ...), condition=%wide.region_2.3_spmd.clone, body=%wide.region_0.2_spmd.clone.sunk | while | flops 4194698 | bytes 13117662 | solution.py:88
  13.4 30.7 %while.39 = (s32[]{:T(128)}, f32[8,1284,128]{2,1,0:T(8,128)}, s32[8,3]{0,1:T(4,128)S(1)}, f32[8,1025,128]{2,1,0:T(8,128)}, s32[]{:T(128)}) while((s32[]{:T(128)}, f32[8,1284,128]{2,1,0:T(8,128)}, s32[8,3]{0,1:T(4,128)S(1)}, f32[8,1025,128]{2,1,0:T(8,128)}, s32[]{:T(128)}) %tuple.117), condition=%wide.while_cond, body=%wide.while_body.sunk | while | flops 2 | bytes 1058409 | solution.py:82
  44.2 4.4 add_reduce_fusion.2
  49.1 10.5 %dynamic_update_slice.9 = f32[4,1024,128]{1,0,2:T(4,128)} dynamic-update-slice(f32[4,1024,128]{1,0,2:T(4,128)} %get-tuple-element.501, f32[1,1024,128]{1,0,2:T(1,128)S(1)} %copy.32, s32[]{:T(128)} %get-tuple-element.500, s32[]{:T(128)} %constant.248.clone.1..sunk, s32[]{:T(128)} %constant.248.clone.1..sunk) | dynamic-update-slice | bytes 1048580 | tf_op jit(solution)/shard_map/while/body/jit(dynamic_update_index_in_dim)/dynamic_update_slice | solution.py:88
  60.8 30.7 %while.39 = (s32[]{:T(128)}, f32[8,1284,128]{2,1,0:T(8,128)}, s32[8,3]{0,1:T(4,128)S(1)}, f32[8,1025,128]{2,1,0:T(8,128)}, s32[]{:T(128)}) while((s32[]{:T(128)}, f32[8,1284,128]{2,1,0:T(8,128)}, s32[8,3]{0,1:T(4,128)S(1)}, f32[8,1025,128]{2,1,0:T(8,128)}, s32[]{:T(128)}) %tuple.117), condition=%wide.while_cond, body=%wide.while_body.sunk | while | flops 2 | bytes 1058409 | solution.py:82
  91.6 4.4 add_reduce_fusion.2
  96.5 10.5 %dynamic_update_slice.9 = f32[4,1024,128]{1,0,2:T(4,128)} dynamic-update-slice(f32[4,1024,128]{1,0,2:T(4,128)} %get-tuple-element.501, f32[1,1024,128]{1,0,2:T(1,128)S(1)} %copy.32, s32[]{:T(128)} %get-tuple-element.500, s32[]{:T(128)} %constant.248.clone.1..sunk, s32[]{:T(128)} %constant.248.clone.1..sunk) | dynamic-update-slice | bytes 1048580 | tf_op jit(solution)/shard_map/while/body/jit(dynamic_update_index_in_dim)/dynamic_update_slice | solution.py:88
  108.2 30.7 %while.39 = (s32[]{:T(128)}, f32[8,1284,128]{2,1,0:T(8,128)}, s32[8,3]{0,1:T(4,128)S(1)}, f32[8,1025,128]{2,1,0:T(8,128)}, s32[]{:T(128)}) while((s32[]{:T(128)}, f32[8,1284,128]{2,1,0:T(8,128)}, s32[8,3]{0,1:T(4,128)S(1)}, f32[8,1025,128]{2,1,0:T(8,128)}, s32[]{:T(128)}) %tuple.117), condition=%wide.while_cond, body=%wide.while_body.sunk | while | flops 2 | bytes 1058409 | solution.py:82
  139.0 4.4 add_reduce_fusion.2
  143.9 10.5 %dynamic_update_slice.9 = f32[4,1024,128]{1,0,2:T(4,128)} dynamic-update-slice(f32[4,1024,128]{1,0,2:T(4,128)} %get-tuple-element.501, f32[1,1024,128]{1,0,2:T(1,128)S(1)} %copy.32, s32[]{:T(128)} %get-tuple-element.500, s32[]{:T(128)} %constant.248.clone.1..sunk, s32[]{:T(128)} %constant.248.clone.1..sunk) | dynamic-update-slice | bytes 1048580 | tf_op jit(solution)/shard_map/while/body/jit(dynamic_update_index_in_dim)/dynamic_update_slice | solution.py:88
  155.6 30.7 %while.39 = (s32[]{:T(128)}, f32[8,1284,128]{2,1,0:T(8,128)}, s32[8,3]{0,1:T(4,128)S(1)}, f32[8,1025,128]{2,1,0:T(8,128)}, s32[]{:T(128)}) while((s32[]{:T(128)}, f32[8,1284,128]{2,1,0:T(8,128)}, s32[8,3]{0,1:T(4,128)S(1)}, f32[8,1025,128]{2,1,0:T(8,128)}, s32[]{:T(128)}) %tuple.117), condition=%wide.while_cond, body=%wide.while_body.sunk | while | flops 2 | bytes 1058409 | solution.py:82
  186.4 4.4 add_reduce_fusion.2
  191.3 10.5 %dynamic_update_slice.9 = f32[4,1024,128]{1,0,2:T(4,128)} dynamic-update-slice(f32[4,1024,128]{1,0,2:T(4,128)} %get-tuple-element.501, f32[1,1024,128]{1,0,2:T(1,128)S(1)} %copy.32, s32[]{:T(128)} %get-tuple-element.500, s32[]{:T(128)} %constant.248.clone.1..sunk, s32[]{:T(128)} %constant.248.clone.1..sunk) | dynamic-update-slice | bytes 1048580 | tf_op jit(solution)/shard_map/while/body/jit(dynamic_update_index_in_dim)/dynamic_update_slice | solution.py:88
  205.8 63.0 %all_to_all.15 = f32[32,4,4,1024]{3,1,2,0:T(4,128)S(1)} all-to-all(f32[32,4,4,1024]{3,1,2,0:T(4,128)S(1)} %bitcast.72), channel_id=1, replica_groups=mesh['gz'=32,'vert'=8] {'gz'}, dimensions={0} | all-to-all | bytes 4194304 | tf_op jit(solution)/shard_map/all_to_all | solution.py:17
  271.2 5.8 %all-to-all-start.1 = ((f32[32,4,4,1024]{3,1,2,0:T(4,128)}), f32[32,4,4,1024]{3,1,2,0:T(4,128)S(1)}, u32[]{:S(2)}, u32[]{:S(2)}) async-start(f32[32,4,4,1024]{3,1,2,0:T(4,128)} %broadcast_in_dim.39), calls=%async_computation.1 | async-start | bytes 4194304 | tf_op jit(solution)/shard_map/all_to_all | solution.py:29
  277.1 50.0 %all-to-all-done.1 = f32[32,4,4,1024]{3,1,2,0:T(4,128)S(1)} async-done(((f32[32,4,4,1024]{3,1,2,0:T(4,128)}), f32[32,4,4,1024]{3,1,2,0:T(4,128)S(1)}, u32[]{:S(2)}, u32[]{:S(2)}) %all-to-all-start.1) | async-done | bytes 2097184 | tf_op jit(solution)/shard_map/all_to_all | solution.py:29
  329.0 11.8 %scatter_fusion = f32[4,128,1024]{2,0,1:T(4,128)S(1)} fusion(f32[4,128,1024]{2,0,1:T(4,128)S(1)} %broadcast_in_dim.38, s32[128]{0:T(128)S(1)} %compare_select_fusion.14, f32[128,4,1024]{2,1,0:T(4,128)} %bitcast.71), kind=kCustom, calls=%fused_computation.1 | custom fusion | bytes 6291968 | tf_op jit(solution)/shard_map/scatter | solution.py:95
  344.4 102.3 %while.38 = (s32[]{:T(128)}, f32[8,1024,128]{2,1,0:T(8,128)}, s32[4]{0:T(128)S(1)}, f32[4,1284,128]{2,1,0:T(8,128)S(1)}, s32[]{:T(128)}, /*index=5*/s32[]{:T(128...) while((s32[]{:T(128)}, f32[8,1024,128]{2,1,0:T(8,128)}, ...), condition=%wide.region_6.7_spmd.clone, body=%wide.region_5.6_spmd.clone.sunk | while | flops 6291827 | bytes 19146876 | solution.py:63
  345.8 16.7 %while.40 = (s32[]{:T(128)}, f32[1284,128]{1,0:T(8,128)S(1)}, s32[8,2]{0,1:T(2,128)S(1)}, f32[8,1025,128]{2,1,0:T(8,128)}, s32[]{:T(128)}) while((s32[]{:T(128)}, f32[1284,128]{1,0:T(8,128)S(1)}, s32[8,2]{0,1:T(2,128)S(1)}, f32[8,1025,128]{2,1,0:T(8,128)}, s32[]{:T(128)}) %tuple.114), condition=%wide.while_cond.1, body=%wide.while_body.1.sunk | while | flops 2 | bytes 1054297 | solution.py:56
  362.6 6.6 %select_add_fusion.2 = f32[8,1024,128]{2,1,0:T(8,128)} fusion(f32[8,1024,128]{2,1,0:T(8,128)} %get-tuple-element.537, f32[8,1025,128]{2,1,0:T(8,128)} %get-tuple-element.444, f32[8]{0:T(128)S(1)} %get-tuple-element.445, f32[8]{0:T(128)S(1)} %get-tuple-element.446, f32[]{:T(128)S(6)} %sqrt.21, pred[]{:T(512)S(6)} %compare.81), kind=kLoop, calls=%fused_computation.24.clone.1 | loop fusion | flops 6291456 | bytes 16777284 | tf_op jit(solution)/shard_map/while/body/eval_jaxpr/add | solution.py:60
  370.5 16.7 %while.40 = (s32[]{:T(128)}, f32[1284,128]{1,0:T(8,128)S(1)}, s32[8,2]{0,1:T(2,128)S(1)}, f32[8,1025,128]{2,1,0:T(8,128)}, s32[]{:T(128)}) while((s32[]{:T(128)}, f32[1284,128]{1,0:T(8,128)S(1)}, s32[8,2]{0,1:T(2,128)S(1)}, f32[8,1025,128]{2,1,0:T(8,128)}, s32[]{:T(128)}) %tuple.114), condition=%wide.while_cond.1, body=%wide.while_body.1.sunk | while | flops 2 | bytes 1054297 | solution.py:56
  387.3 7.8 %select_add_fusion.2 = f32[8,1024,128]{2,1,0:T(8,128)} fusion(f32[8,1024,128]{2,1,0:T(8,128)} %get-tuple-element.537, f32[8,1025,128]{2,1,0:T(8,128)} %get-tuple-element.444, f32[8]{0:T(128)S(1)} %get-tuple-element.445, f32[8]{0:T(128)S(1)} %get-tuple-element.446, f32[]{:T(128)S(6)} %sqrt.21, pred[]{:T(512)S(6)} %compare.81), kind=kLoop, calls=%fused_computation.24.clone.1 | loop fusion | flops 6291456 | bytes 16777284 | tf_op jit(solution)/shard_map/while/body/eval_jaxpr/add | solution.py:60
  396.4 16.7 %while.40 = (s32[]{:T(128)}, f32[1284,128]{1,0:T(8,128)S(1)}, s32[8,2]{0,1:T(2,128)S(1)}, f32[8,1025,128]{2,1,0:T(8,128)}, s32[]{:T(128)}) while((s32[]{:T(128)}, f32[1284,128]{1,0:T(8,128)S(1)}, s32[8,2]{0,1:T(2,128)S(1)}, f32[8,1025,128]{2,1,0:T(8,128)}, s32[]{:T(128)}) %tuple.114), condition=%wide.while_cond.1, body=%wide.while_body.1.sunk | while | flops 2 | bytes 1054297 | solution.py:56
  413.1 7.8 %select_add_fusion.2 = f32[8,1024,128]{2,1,0:T(8,128)} fusion(f32[8,1024,128]{2,1,0:T(8,128)} %get-tuple-element.537, f32[8,1025,128]{2,1,0:T(8,128)} %get-tuple-element.444, f32[8]{0:T(128)S(1)} %get-tuple-element.445, f32[8]{0:T(128)S(1)} %get-tuple-element.446, f32[]{:T(128)S(6)} %sqrt.21, pred[]{:T(512)S(6)} %compare.81), kind=kLoop, calls=%fused_computation.24.clone.1 | loop fusion | flops 6291456 | bytes 16777284 | tf_op jit(solution)/shard_map/while/body/eval_jaxpr/add | solution.py:60
  422.2 16.7 %while.40 = (s32[]{:T(128)}, f32[1284,128]{1,0:T(8,128)S(1)}, s32[8,2]{0,1:T(2,128)S(1)}, f32[8,1025,128]{2,1,0:T(8,128)}, s32[]{:T(128)}) while((s32[]{:T(128)}, f32[1284,128]{1,0:T(8,128)S(1)}, s32[8,2]{0,1:T(2,128)S(1)}, f32[8,1025,128]{2,1,0:T(8,128)}, s32[]{:T(128)}) %tuple.114), condition=%wide.while_cond.1, body=%wide.while_body.1.sunk | while | flops 2 | bytes 1054297 | solution.py:56
  439.0 7.8 %select_add_fusion.2 = f32[8,1024,128]{2,1,0:T(8,128)} fusion(f32[8,1024,128]{2,1,0:T(8,128)} %get-tuple-element.537, f32[8,1025,128]{2,1,0:T(8,128)} %get-tuple-element.444, f32[8]{0:T(128)S(1)} %get-tuple-element.445, f32[8]{0:T(128)S(1)} %get-tuple-element.446, f32[]{:T(128)S(6)} %sqrt.21, pred[]{:T(512)S(6)} %compare.81), kind=kLoop, calls=%fused_computation.24.clone.1 | loop fusion | flops 6291456 | bytes 16777284 | tf_op jit(solution)/shard_map/while/body/eval_jaxpr/add | solution.py:60
  446.8 5.4 %copy.18 = f32[8,1024,128]{1,2,0:T(8,128)} copy(f32[8,1024,128]{2,1,0:T(8,128)} %get-tuple-element.200) | data formatting | bytes 8388608 | tf_op jit(solution)/shard_map/while | solution.py:63
  452.1 4.7 copy.19
  456.9 4.5 all-to-all-start.2
  462.1 48.3 %all-to-all-done.2 = f32[8,8,16,1024]{3,2,1,0:T(8,128)} async-done(((f32[8,8,16,1024]{3,2,1,0:T(8,128)}), f32[8,8,16,1024]{3,2,1,0:T(8,128)}, u32[]{:S(2)}, u32[]{:S(2)}) %all-to-all-start.2) | async-done | bytes 4194336 | tf_op jit(solution)/shard_map/all_to_all | solution.py:17
  (270 shorter events, 214.0 us)
Async XLA Ops:
  7.3 4.8 copy-start.2
  205.8 63.5 %copy-start.1 = (f32[4,4,1024]{2,1,0:T(4,128)S(1)}, f32[4,4,1024]{2,1,0:T(4,128)}, u32[]{:S(2)}) copy-start(f32[4,4,1024]{2,1,0:T(4,128)} %param.11) | copy-start | bytes 196612
  271.2 55.9 %all-to-all-start.1 = ((f32[32,4,4,1024]{3,1,2,0:T(4,128)}), f32[32,4,4,1024]{3,1,2,0:T(4,128)S(1)}, u32[]{:S(2)}, u32[]{:S(2)}) async-start(f32[32,4,4,1024]{3,1,2,0:T(4,128)} %broadcast_in_dim.39), calls=%async_computation.1 | async-start | bytes 4194304 | tf_op jit(solution)/shard_map/all_to_all | solution.py:29
  327.1 1.3 copy-start
  456.9 53.6 %all-to-all-start.2 = ((f32[8,8,16,1024]{3,2,1,0:T(8,128)}), f32[8,8,16,1024]{3,2,1,0:T(8,128)}, u32[]{:S(2)}, u32[]{:S(2)}) async-start(f32[8,8,16,1024]{3,2,1,0:T(8,128)} %copy.19), calls=%async_computation.2 | async-start | bytes 8388608 | tf_op jit(solution)/shard_map/all_to_all | solution.py:17
where the time goes:
time: 519 us; the launch traced here: 514 us
  local copies, waits for them, and re-layouts  282 us (54%)
  waiting for transfers between devices  98.4 us (19%)
  blocking collectives  63 us (12%)
  other arithmetic  53.8 us (10%)
  starting transfers between devices  10.4 us (2%)
  loops' own time  5.7 us (1%)
    gather x192, local copies, waits for them, and re-layouts  190 us
    all_to_all x1, blocking collectives, sent_and_summed(): tiles = lax.all_to_all(in_blocks(value, dim, peers), axis, 0, 0, tiled=True)  63 us
    all_to_all x1, waiting for transfers between devices, sent_to_all(): return lax.all_to_all(copies, axis, split_axis=0, concat_axis=0, tiled=True)  50 us
    all_to_all x1, waiting for transfers between devices, sent_and_summed(): tiles = lax.all_to_all(in_blocks(value, dim, peers), axis, 0, 0, tiled=True)  48.3 us
    dynamic_update_slice x8, local copies, waits for them, and re-layouts, per_device(): partial_cols = lax.map(project, angle_index)  43.7 us
    add x4, other arithmetic, add_view(): return (running + weight * contrib, None)  29.9 us
    reduce_sum x4, other arithmetic, project(): return weight * jnp.sum(contrib, axis=0)  17.6 us
    scatter x1, local copies, waits for them, and re-layouts, per_device(): back = jnp.zeros_like(full_rows).at[:, detector_rows, :].set(full_rows)  11.8 us
  transfers between devices with their start and end apart: 2, of which 2 were waited for; matrix products, arithmetic and copies ran while one was open for 0% of the time, Pallas kernels for 0%

commit v1 on v0

v1 whole, which is shorter than its diff:
```python
import jax
import jax.numpy as jnp
from jax import lax
from jax.experimental import pallas as pl
from jax.experimental.pallas import tpu as pltpu
from jax.sharding import PartitionSpec as P

L = 128
CHIPS = 16
VERT = 8
VIEWS = 32
MID = 1
EXT = 56
F32 = jnp.float32
HIGH = lax.Precision.HIGHEST


def at(gz, vert):
    return {"gz": gz, "vert": vert}


def lane_iota(shape=(8, L)):
    return lax.broadcasted_iota(jnp.int32, shape, len(shape) - 1)


def sub_iota(shape=(8, L)):
    return lax.broadcasted_iota(jnp.int32, shape, len(shape) - 2)


def visit(i, p):
    step = lax.div(i, 2)
    far = lax.div(step + 1, 2)
    dz = jnp.where(lax.rem(step, 2) == 1, far, 8 - far)
    z = lax.rem(lax.div(p, 2) + dz, 8)
    return z * 2 + lax.rem(p + i, 2)


def row_of(ref, r):
    return jnp.broadcast_to(ref[pl.ds(r, 1), :], (8, L))


def extend(x, ext, base):
    lane = lane_iota()
    zero = jnp.zeros((8, L), F32)
    r1, r2, r3 = (pltpu.roll(x, L - n, 1) for n in (1, 2, 3))
    parts = (
        x,
        jnp.where(lane < 127, r1, zero),
        jnp.where(lane < 126, r2, zero),
        jnp.where(lane < 126, x, zero),
        jnp.where(lane == 126, zero, r1),
        r2,
        jnp.where(lane == 125, zero, r3),
    )
    for n, value in enumerate(parts):
        ext[base + 8 * n : base + 8 * n + 8, :] = value


def project_slab(chunk, slab, ext, phi_t, tab, part):
    lane = lane_iota()
    for zz in range(8):
        extend(chunk[zz], ext, zz * EXT)
    for v in range(VIEWS):
        acc = None
        for zz in range(8):
            off = tab[0, v, slab * 8 + zz] + zz * EXT
            a = ext[pl.ds(off, 8), :]
            b = ext[pl.ds(off + 1, 8), :]
            phi = row_of(phi_t.at[v], slab * 8 + zz)
            term = a + phi * (b - a)
            acc = term if acc is None else acc + term
        kc = tab[1, v, slab * 8]
        pos = lane + kc
        moved = pltpu.roll(acc, (L - kc) & (L - 1), 1)
        part[v] += jnp.where((pos >= -2) & (pos < L), moved, 0.0)


def backproject_slab(slab, bw, ext, phi_t, tab, out):
    lane = lane_iota()
    for v in range(VIEWS):
        kc = tab[3, v, slab * 8]
        row = bw[v]
        for n in range(3):
            pos = lane + (kc + n)
            moved = pltpu.roll(row, (2 * L - kc - n) & (L - 1), 1)
            ext[v * 24 + 8 * n : v * 24 + 8 * n + 8, :] = jnp.where((pos >= 0) & (pos < L), moved, 0.0)
    for zz in range(8):
        acc = None
        for v in range(VIEWS):
            off = tab[2, v, slab * 8 + zz] + v * 24
            b = ext[pl.ds(off, 8), :]
            a = ext[pl.ds(off + 1, 8), :]
            phi = row_of(phi_t.at[v], slab * 8 + zz)
            term = a + phi * (b - a)
            acc = term if acc is None else acc + term
        out[zz] = acc


def to_tiles(read, batch, turned, tiles):
    for t in range(8):
        turned[t * L : (t + 1) * L, 0:batch] = jnp.transpose(read(t))
    for r in range(8):
        tiles[r * batch : (r + 1) * batch, :] = jnp.transpose(turned[pl.ds(r, L, stride=8), 0:batch])


def one_hot(dr, bit):
    lane = lane_iota((8, L))
    wide = jnp.broadcast_to(dr, (8, L))
    halves = []
    for half in range(2):
        src = half * 64 + (lane // 8) * 4 + lane % 4
        got = jnp.take_along_axis(wide, src, axis=1, mode="promise_in_bounds")
        got = jnp.where((lane // 4) % 2 == bit, got, -1)
        halves.append(jnp.broadcast_to(got[0:1], (L, L)))
    row = lax.broadcasted_iota(jnp.int32, (L, 2 * L), 0)
    return (jnp.concatenate(halves, axis=1) == row).astype(F32)


def kernel(
    volume, angles, det, measured,
    grad_in, res_in,
    vb, mbuf, m16, turned, tiles, xsend, xin, abuf, sf, wt, tab_v, phi_t, ext, ext_b,
    part, pin, bw, mtiles, mi, mr, m2, msend, m3, rsend, r2, rs2, r3, xres, gsend, tab,
    loc_sem, vol_send, vol_recv, ang_send, ang_recv, part_send, part_recv,
    mid_send, mid_recv, grad_send, grad_recv,
):
    gz, vert = lax.axis_index("gz"), lax.axis_index("vert")
    p, core = lax.div(gz, 2), lax.rem(gz, 2)
    barrier = pltpu.get_barrier_semaphore()

    load_v = pltpu.make_async_copy(volume.at[:, pl.ds(pl.multiple_of(vert * 16, 16), 16), :], vb, loc_sem.at[0])
    load_m = pltpu.make_async_copy(measured, mbuf, loc_sem.at[1])
    load_v.start()
    load_m.start()

    def greet_gz(i, _):
        pl.semaphore_signal(barrier, inc=1, device_id=at(lax.rem(gz + i, 32), vert))
        return 0

    def greet_vert(i, _):
        pl.semaphore_signal(barrier, inc=1, device_id=at(gz, lax.rem(vert + i, VERT)))
        return 0

    lax.fori_loop(1, 32, greet_gz, 0)
    lax.fori_loop(1, VERT, greet_vert, 0)

    sub = sub_iota()
    slope = jnp.zeros((8, L), jnp.int32)
    for i in range(4):
        slope = jnp.where(sub % 4 == i, jnp.full((8, L), 2 * angles[i] - 512), slope)
    abuf[vert] = slope
    part[...] = jnp.zeros_like(part)

    load_m.wait()
    for a in range(4):
        m16[4 * a : 4 * a + 4, :] = mbuf[a]
    to_tiles(lambda t: m16[:, t * L : (t + 1) * L], 16, turned, mtiles)
    load_v.wait()
    to_tiles(lambda t: vb[:, :, t * L : (t + 1) * L].reshape(L, L), L, turned, tiles)

    def gather_rows(q, _):
        for zz in range(8):
            xsend[q, zz] = tiles[pl.ds(zz * 16 + q, 8, stride=L), :]
        return 0

    lax.fori_loop(0, CHIPS, gather_rows, 0)
    for zz in range(8):
        xin[p, zz] = xsend[p, zz]

    pl.semaphore_wait(barrier, 31 + 7)

    def send_angles(i, _):
        pltpu.make_async_remote_copy(
            abuf.at[vert], abuf.at[vert], ang_send, ang_recv, device_id=at(gz, lax.rem(vert + i, VERT))
        ).start()
        return 0

    lax.fori_loop(1, VERT, send_angles, 0)

    def measured_chunk(q):
        return mtiles.at[pl.ds(pl.multiple_of(lax.rem(q, 8) * 16 + lax.div(q, 8) * 8, 8), 8)]

    def send_measured(i, _):
        q = lax.rem(p + i, CHIPS)

        @pl.when(q * 2 + MID != gz)
        def _():
            pltpu.make_async_remote_copy(
                measured_chunk(q), mi.at[gz], mid_send.at[0], mid_recv.at[0], device_id=at(q * 2 + MID, vert)
            ).start()

        return 0

    lax.fori_loop(0, CHIPS, send_measured, 0)

    def vol_copy(i):
        q = visit(i, p)
        return pltpu.make_async_remote_copy(
            xsend.at[q], xin.at[p], vol_send, vol_recv.at[p], device_id=at(q * 2 + core, vert)
        )

    def send_volume(i, _):
        vol_copy(i).start()
        return 0

    lax.fori_loop(1, CHIPS, send_volume, 0)

    @pl.when(core == MID)
    def _():
        mi[gz] = measured_chunk(p)[...]

    pltpu.make_async_copy(abuf.at[pl.ds(0, 7)], abuf.at[pl.ds(0, 7)], ang_recv).wait()
    for g in range(4):
        tab_v[0, 8 * g : 8 * g + 8, :] = jnp.where(sub < 4, abuf[2 * g], abuf[2 * g + 1])
    s = tab_v[0]
    sf[...] = s.astype(F32)
    slope_value = sf[...] * (1.0 / 512)
    wt[...] = jnp.sqrt(1.0 + slope_value * slope_value)
    lane = lane_iota((VIEWS, L))
    first = 16 * (lane // 8) + 8 * core - 128
    ends = ((first * s) >> 9, ((first + 7) * s) >> 9)
    k_min, k_max = jnp.minimum(*ends), jnp.maximum(*ends)
    k = ((first + lane % 8) * s) >> 9
    kc = jnp.where(k_min < 0, jnp.minimum(k_min >> 3, -2), k_min >> 3)
    tab_v[0] = k - 8 * kc + jnp.where(k_min < 0, 24, 0)
    tab_v[1] = kc
    kb = (-k_max - 1) >> 3
    tab_v[2] = -k - 1 - 8 * kb
    tab_v[3] = kb
    to_smem = pltpu.make_async_copy(tab_v, tab, loc_sem.at[2])
    to_smem.start()

    def fill_phi(v, _):
        sv = row_of(sf, v)
        for slab in range(CHIPS):
            q = (16 * slab + 8 * core - 128 + sub).astype(F32) * sv * (1.0 / 512)
            phi_t[v, slab * 8 : slab * 8 + 8, :] = q - jnp.floor(q)
        return 0

    lax.fori_loop(0, VIEWS, fill_phi, 0)
    to_smem.wait()

    def project_step(i, _):
        q = visit(i, p)

        @pl.when(i > 0)
        def _():
            pltpu.make_async_copy(xin.at[q], xin.at[q], vol_recv.at[q]).wait()

        project_slab(xin.at[q], q, ext, phi_t, tab, part)

        @pl.when((core == MID) & (i == 3))
        def _():
            pltpu.make_async_copy(mi.at[pl.ds(0, 31)], mi.at[pl.ds(0, 31)], mid_recv.at[0]).wait()
            got = mi[...].reshape(2 * L, L)
            for bit in range(2):
                rows = jnp.dot(one_hot(det[...], bit), got, precision=HIGH, preferred_element_type=F32)
                mr[:, bit] = rows.reshape(VERT, 16, L)

            def send(n, _):
                w = lax.rem(vert + n, VERT)
                pltpu.make_async_remote_copy(
                    mr.at[w], m2.at[vert], mid_send.at[1], mid_recv.at[1], device_id=at(gz, w)
                ).start()
                return 0

            lax.fori_loop(1, VERT, send, 0)
            m2[vert] = mr[vert]

        @pl.when((core == MID) & (i == 7))
        def _():
            pltpu.make_async_copy(m2.at[pl.ds(0, 7)], m2.at[pl.ds(0, 7)], mid_recv.at[1]).wait()
            flat = m2.reshape(256, L)
            for q in range(CHIPS):
                msend[q] = flat[pl.ds(q, 16, stride=16), :]

            def send(n, _):
                w = lax.rem(p + n, CHIPS)
                pltpu.make_async_remote_copy(
                    msend.at[w], m3.at[p], mid_send.at[2], mid_recv.at[2], device_id=at(w * 2 + MID, vert)
                ).start()
                return 0

            lax.fori_loop(1, CHIPS, send, 0)
            m3[p] = msend[p]

        return 0

    lax.fori_loop(0, CHIPS, project_step, 0)

    for v in range(VIEWS):
        part[v] = part[v] * row_of(wt, v)

    @pl.when(core == MID)
    def _():
        pltpu.make_async_copy(m3.at[pl.ds(0, 15)], m3.at[pl.ds(0, 15)], mid_recv.at[2]).wait()
        flat = m3.reshape(256, L)
        for v in range(VIEWS):
            w, pair, bit = v // 4, (v % 4) // 2, v % 2
            part[v] = part[v] - flat[pl.ds(pair * 128 + 2 * w + bit, 8, stride=16), :]

    swap = pltpu.make_async_remote_copy(part, pin, part_send, part_recv, device_id=at(gz + 1 - 2 * core, vert))
    swap.start()
    swap.wait()
    for v in range(VIEWS):
        value = (part[v] + pin[v]) * (1.0 / 16)
        pin[v] = value
        bw[v] = value * row_of(wt, v) * (VIEWS**-0.5)

    flat_res = pin.reshape(VIEWS * 8, L)
    for b in range(8):
        for bit in range(2):
            rsend[b, 8 * bit : 8 * bit + 8, :] = flat_res[pl.ds((2 * core + bit) * 8 + b, 8, stride=32), :]

    def send_residual(b, _):
        q = core * 8 + b

        @pl.when(q * 2 + MID != gz)
        def _():
            pltpu.make_async_remote_copy(
                rsend.at[b], r2.at[p], mid_send.at[3], mid_recv.at[3], device_id=at(q * 2 + MID, vert)
            ).start()

        return 0

    lax.fori_loop(0, 8, send_residual, 0)
    own_mid = (core == MID) & (lax.div(p, 8) == MID)

    @pl.when(own_mid)
    def _():
        r2[p] = rsend[lax.rem(p, 8)]

    def grad_copy(q):
        return pltpu.make_async_remote_copy(
            gsend.at[q], grad_in.at[p], grad_send, grad_recv, device_id=at(q * 2 + core, vert)
        )

    def back_step(i, _):
        q = visit(CHIPS - 1 - i, p)
        backproject_slab(q, bw, ext_b, phi_t, tab, gsend.at[q])

        @pl.when(i < CHIPS - 1)
        def _():
            grad_copy(q).start()

        @pl.when((core == MID) & (i == 3))
        def _():
            @pl.when(own_mid)
            def _():
                pltpu.make_async_copy(r2.at[pl.ds(0, 15)], r2.at[pl.ds(0, 15)], mid_recv.at[3]).wait()

            @pl.when(jnp.logical_not(own_mid))
            def _():
                pltpu.make_async_copy(r2, r2, mid_recv.at[3]).wait()

            flat = r2.reshape(256, L)
            for w in range(VERT):
                for bit in range(2):
                    rs2[w, bit] = flat[pl.ds(bit * 8 + w, 16, stride=16), :]

            def send(n, _):
                w = lax.rem(vert + n, VERT)
                pltpu.make_async_remote_copy(
                    rs2.at[w], r3.at[vert], mid_send.at[4], mid_recv.at[4], device_id=at(gz, w)
                ).start()
                return 0

            lax.fori_loop(1, VERT, send, 0)
            r3[vert] = rs2[vert]

        @pl.when((core == MID) & (i == 7))
        def _():
            pltpu.make_async_copy(r3.at[pl.ds(0, 7)], r3.at[pl.ds(0, 7)], mid_recv.at[4]).wait()
            total = None
            for bit in range(2):
                rows = r3[:, bit].reshape(L, L)
                hot = jnp.transpose(one_hot(det[...], bit))
                out = jnp.dot(hot, rows, precision=HIGH, preferred_element_type=F32)
                total = out if total is None else total + out
            xres[...] = total.reshape(32, 8, L)

            def send(n, _):
                w = lax.rem(gz + n, 32)
                pltpu.make_async_remote_copy(
                    xres.at[w], res_in.at[p], mid_send.at[5], mid_recv.at[5], device_id=at(w, vert)
                ).start()
                return 0

            lax.fori_loop(1, 32, send, 0)
            pltpu.make_async_copy(xres.at[gz], res_in.at[p], loc_sem.at[3]).start()

        return 0

    lax.fori_loop(0, CHIPS, back_step, 0)
    own_grad = pltpu.make_async_copy(gsend.at[p], grad_in.at[p], loc_sem.at[4])
    own_grad.start()

    pltpu.make_async_copy(abuf.at[pl.ds(0, 7)], abuf.at[pl.ds(0, 7)], ang_send).wait()
    pltpu.make_async_copy(xin.at[pl.ds(0, 15)], xin.at[pl.ds(0, 15)], vol_send).wait()

    @pl.when(core == MID)
    def _():
        pltpu.make_async_copy(mi.at[pl.ds(0, 15)], mi.at[pl.ds(0, 15)], mid_send.at[0]).wait()
        pltpu.make_async_copy(m2.at[pl.ds(0, 7)], m2.at[pl.ds(0, 7)], mid_send.at[1]).wait()
        pltpu.make_async_copy(m3.at[pl.ds(0, 15)], m3.at[pl.ds(0, 15)], mid_send.at[2]).wait()
        pltpu.make_async_copy(r3.at[pl.ds(0, 7)], r3.at[pl.ds(0, 7)], mid_send.at[4]).wait()
        pltpu.make_async_copy(xres.at[pl.ds(0, 31)], xres.at[pl.ds(0, 31)], mid_send.at[5]).wait()
        pltpu.make_async_copy(xres.at[gz], res_in.at[p], loc_sem.at[3]).wait()
        pltpu.make_async_copy(res_in.at[pl.ds(0, 15)], res_in.at[pl.ds(0, 15)], mid_recv.at[5]).wait()

    @pl.when(core != MID)
    def _():
        pltpu.make_async_copy(mi.at[pl.ds(0, 16)], mi.at[pl.ds(0, 16)], mid_send.at[0]).wait()
        pltpu.make_async_copy(res_in, res_in, mid_recv.at[5]).wait()

    @pl.when(own_mid)
    def _():
        pltpu.make_async_copy(rsend.at[pl.ds(0, 7)], rsend.at[pl.ds(0, 7)], mid_send.at[3]).wait()

    @pl.when(jnp.logical_not(own_mid))
    def _():
        pltpu.make_async_copy(rsend, rsend, mid_send.at[3]).wait()

    own_grad.wait()
    pltpu.make_async_copy(gsend.at[pl.ds(0, 15)], gsend.at[pl.ds(0, 15)], grad_send).wait()
    pltpu.make_async_copy(grad_in.at[pl.ds(0, 15)], grad_in.at[pl.ds(0, 15)], grad_recv).wait()


def exchange(volume, angles, det, measured):
    dma = pltpu.SemaphoreType.DMA
    any_space = pl.BlockSpec(memory_space=pl.ANY)
    vmem = lambda *dims, dtype=F32: pltpu.VMEM(dims, dtype)
    scratch = [
        vmem(8, 16, 1024), vmem(4, 4, 1024), vmem(16, 1024), vmem(1024, L), vmem(1024, L),
        vmem(CHIPS, 8, 8, L), vmem(CHIPS, 8, 8, L), vmem(VERT, 8, L, dtype=jnp.int32), vmem(VIEWS, L), vmem(VIEWS, L),
        vmem(4, VIEWS, L, dtype=jnp.int32), vmem(VIEWS, L, L), vmem(8 * EXT, L), vmem(VIEWS * 24, L),
        vmem(VIEWS, 8, L), vmem(VIEWS, 8, L), vmem(VIEWS, 8, L), vmem(L, L), vmem(32, 8, L), vmem(VERT, 2, 16, L),
        vmem(VERT, 2, 16, L), vmem(CHIPS, 16, L), vmem(CHIPS, 16, L), vmem(8, 16, L), vmem(CHIPS, 16, L),
        vmem(VERT, 2, 16, L), vmem(VERT, 2, 16, L), vmem(32, 8, L), vmem(CHIPS, 8, 8, L),
        pltpu.SMEM((4, VIEWS, L), jnp.int32),
        dma((5,)), dma, dma((CHIPS,)), dma, dma, dma, dma, dma((6,)), dma((6,)), dma, dma,
    ]
    return pl.pallas_call(
        kernel,
        out_shape=[jax.ShapeDtypeStruct((CHIPS, 8, 8, L), F32), jax.ShapeDtypeStruct((CHIPS, 8, L), F32)],
        in_specs=[
            any_space,
            pl.BlockSpec(memory_space=pltpu.SMEM),
            pl.BlockSpec(memory_space=pltpu.VMEM),
            any_space,
        ],
        out_specs=[any_space, any_space],
        scratch_shapes=scratch,
        compiler_params=pltpu.CompilerParams(collective_id=0, has_side_effects=True, vmem_limit_bytes=40 * 2**20),
        name="exchange",
    )(volume, angles, det, measured)


def finish_kernel(grad_in, res_in, res_out, grad_out, turned):
    for r in range(8):
        both = jnp.concatenate([res_in[r], res_in[8 + r]], axis=0)
        turned[pl.ds(r, L, stride=8), 0:16] = jnp.transpose(both)
    for t in range(8):
        rows = jnp.transpose(turned[t * L : (t + 1) * L, 0:16])
        for a in range(4):
            res_out[a, :, t * L : (t + 1) * L] = rows[4 * a : 4 * a + 4]
    flat = grad_in.reshape(CHIPS * 64, L)
    for r in range(8):
        rows = [flat[pl.ds(zz * 8 + r, 16, stride=64), :] for zz in range(8)]
        turned[pl.ds(r, L, stride=8), :] = jnp.transpose(jnp.concatenate(rows, axis=0))
    for t in range(8):
        grad_out[:, :, t * L : (t + 1) * L] = jnp.transpose(turned[t * L : (t + 1) * L, :]).reshape(8, 16, L)


def finish(grad_in, res_in):
    return pl.pallas_call(
        finish_kernel,
        out_shape=[jax.ShapeDtypeStruct((4, 4, 1024), F32), jax.ShapeDtypeStruct((8, 16, 1024), F32)],
        in_specs=[pl.BlockSpec(memory_space=pltpu.VMEM)] * 2,
        out_specs=[pl.BlockSpec(memory_space=pltpu.VMEM)] * 2,
        scratch_shapes=[pltpu.VMEM((1024, L), F32)],
        name="finish",
    )(grad_in, res_in)


def per_device(volume, angle_index, detector_rows, measured):
    grad_in, res_in = exchange(volume, angle_index, detector_rows.reshape(1, L), measured)
    residual, gradient = finish(grad_in, res_in)
    return residual, gradient


def solution(mesh):
    in_specs = (P("gz", None, None), P("vert"), P(), P("vert", "gz", None))
    out_specs = (P("vert", "gz", None), P("gz", "vert", None))
    return jax.shard_map(per_device, mesh=mesh, in_specs=in_specs, out_specs=out_specs, check_vma=False)
```

time: 519 us -> 63.2 us (0.12)
  local copies, waits for them, and re-layouts: 282 us -> 5.74 us
  waiting for transfers between devices: 98.4 us -> 0 us
  blocking collectives: 63 us -> 0 us
  Pallas kernels: 0 us -> 56.1 us
  other arithmetic: 53.8 us -> 0 us
  starting transfers between devices: 10.4 us -> 0 us
  loops' own time: 5.7 us -> 0 us
    gather x193 -> x0, local copies, waits for them, and re-layouts: 193 us -> none
    all_to_all x2 -> x0, waiting for transfers between devices: 98.4 us -> none  [the longest x1 50 us: sent_to_all(): return lax.all_to_all(copies, axis, split_axis=0, concat_axis=0, tiled=True)]
    all_to_all x1 -> x0, blocking collectives: 63 us -> none  [sent_and_summed(): tiles = lax.all_to_all(in_blocks(value, dim, peers), axis, 0, 0, tiled=True)]
    pallas_call x0 -> x2, Pallas kernels: none -> 56.1 us  [the longest x1 53.4 us: exchange(): pl.pallas_call(kernel, out_shape=[jax.ShapeDtypeStruct((CHIPS, 8, 8, L),...]
    dynamic_update_slice x8 -> x0, local copies, waits for them, and re-layouts: 43.7 us -> none  [per_device(): partial_cols = lax.map(project, angle_index)]
    add x4 -> x0, other arithmetic: 29.9 us -> none  [add_view(): return (running + weight * contrib, None)]
    reduce_sum x6 -> x0, other arithmetic: 20.7 us -> none  [the longest x4 17.6 us: project(): return weight * jnp.sum(contrib, axis=0)]
    scatter x1 -> x0, local copies, waits for them, and re-layouts: 11.8 us -> none  [per_device(): back = jnp.zeros_like(full_rows).at[:, detector_rows, :].set(full_rows)]
  transfers between devices with their start and end apart: 2 -> 0, of which waited for: 2 -> 0; matrix products, arithmetic and copies ran while one was open for 0% -> 0% of each run, Pallas kernels for 0% -> 0%
where the time goes in v1:
time: 63.2 us; the launch traced here: 62.5 us
  Pallas kernels  56.1 us (89%)
  local copies, waits for them, and re-layouts  5.74 us (9%)
  between operations  0.66 us (1%)
    pallas_call x1, Pallas kernels, exchange(): pl.pallas_call(kernel, out_shape=[jax.ShapeDtypeStruct((CHIPS, 8, 8, L),...  53.4 us
    unnamed x12, local copies, waits for them, and re-layouts  5.74 us
    pallas_call x1, Pallas kernels, finish(): pl.pallas_call(finish_kernel, out_shape=[jax.ShapeDtypeStruct((4, 4, 1024...  2.7 us

profile of v1, /device:TPU:1, one launch (start us, length us, event | category | flops | bytes accessed | tf_op | source)
XLA Modules:
  0.0 62.5 jit_solution(3234136770028668320)
XLA Ops:
  0.6 0.0 copy-start
  0.6 2.2 %copy-done = f32[8,128,1024]{2,1,0:T(8,128)S(1)} copy-done((f32[8,128,1024]{2,1,0:T(8,128)S(1)}, f32[8,128,1024]{2,1,0:T(8,128)}, u32[]{:S(2)}) %copy-start) | copy-done | bytes 4194328
  2.8 0.0 copy-start.2
  2.8 0.8 %copy-done.2 = f32[4,4,1024]{2,1,0:T(4,128)S(1)} copy-done((f32[4,4,1024]{2,1,0:T(4,128)S(1)}, f32[4,4,1024]{2,1,0:T(4,128)}, u32[]{:S(2)}) %copy-start.2) | copy-done | bytes 65560
  3.7 0.0 copy-start.4
  3.7 0.7 %copy-done.4 = s32[4]{0:T(128)S(1)} copy-done((s32[4]{0:T(128)S(1)}, s32[4]{0:T(128)}, u32[]{:S(2)}) %copy-start.4) | copy-done | bytes 40
  4.3 0.0 copy-start.5
  4.3 0.7 %copy-done.5 = s32[128]{0:T(128)S(1)} copy-done((s32[128]{0:T(128)S(1)}, s32[128]{0:T(128)}, u32[]{:S(2)}) %copy-start.5) | copy-done | bytes 536
  5.0 53.4 %exchange.1 = (f32[16,8,8,128]{3,2,1,0:T(8,128)S(1)}, f32[16,8,128]{2,1,0:T(8,128)S(1)}) custom-call(f32[8,128,1024]{2,1,0:T(8,128)S(1)} %copy-done, s32[4]{0:T(128)S(1)} %copy-done.4, s32[1,128]{1,0:T(1,128)S(1)} %bitcast.1, f32[4,4,1024]{2,1,0:T(4,128)S(1)} %copy-done.2), custom_call_target="tpu_custom_call" | custom-call | tf_op jit(solution)/shard_map/exchange/pallas_call | solution.py:443
  58.4 0.0 copy-start.1
  58.4 0.8 %copy-done.1 = f32[16,8,8,128]{3,2,1,0:T(8,128)} copy-done((f32[16,8,8,128]{3,2,1,0:T(8,128)}, f32[16,8,8,128]{3,2,1,0:T(8,128)S(1)}, u32[]{:S(2)}) %copy-start.1) | copy-done | bytes 524312
  59.2 0.0 copy-start.3
  59.2 0.6 copy-done.3
  59.8 2.7 %finish.1 = (f32[4,4,1024]{2,1,0:T(4,128)}, f32[8,16,1024]{2,1,0:T(8,128)}) custom-call(f32[16,8,8,128]{3,2,1,0:T(8,128)} %copy-done.1, f32[16,8,128]{2,1,0:T(8,128)} %copy-done.3), custom_call_target="tpu_custom_call" | custom-call | tf_op jit(solution)/shard_map/finish/pallas_call | solution.py:476
Async XLA Ops:
  0.6 2.2 %copy-start = (f32[8,128,1024]{2,1,0:T(8,128)S(1)}, f32[8,128,1024]{2,1,0:T(8,128)}, u32[]{:S(2)}) copy-start(f32[8,128,1024]{2,1,0:T(8,128)} %volume.1) | copy-start | bytes 12582916
  2.8 0.8 %copy-start.2 = (f32[4,4,1024]{2,1,0:T(4,128)S(1)}, f32[4,4,1024]{2,1,0:T(4,128)}, u32[]{:S(2)}) copy-start(f32[4,4,1024]{2,1,0:T(4,128)} %measured.1) | copy-start | bytes 196612
  3.7 0.7 %copy-start.4 = (s32[4]{0:T(128)S(1)}, s32[4]{0:T(128)}, u32[]{:S(2)}) copy-start(s32[4]{0:T(128)} %angles.1) | copy-start | bytes 52
  4.3 0.7 %copy-start.5 = (s32[128]{0:T(128)S(1)}, s32[128]{0:T(128)}, u32[]{:S(2)}) copy-start(s32[128]{0:T(128)} %param.6) | copy-start | bytes 1540
  58.4 0.8 %copy-start.1 = (f32[16,8,8,128]{3,2,1,0:T(8,128)}, f32[16,8,8,128]{3,2,1,0:T(8,128)S(1)}, u32[]{:S(2)}) copy-start(f32[16,8,8,128]{3,2,1,0:T(8,128)S(1)} %get-tuple-element.4.grad_in) | copy-start | bytes 1572868
  59.2 0.6 %copy-start.3 = (f32[16,8,128]{2,1,0:T(8,128)}, f32[16,8,128]{2,1,0:T(8,128)S(1)}, u32[]{:S(2)}) copy-start(f32[16,8,128]{2,1,0:T(8,128)S(1)} %get-tuple-element.5.res_in) | copy-start | bytes 196612

commit v2 on v1

--- a/solution.py
+++ b/solution.py
@@ -9,9 +9,14 @@
 CHIPS = 16
 VERT = 8
 VIEWS = 32
+GROUP = 8
+AT_ONCE = 2
+FORWARD_AT = 6
+BACK_AT = 9
 MID = 1
 EXT = 56
 F32 = jnp.float32
+ALL_VMEM = 62 * 2**20
 HIGH = lax.Precision.HIGHEST
 
 
@@ -56,44 +61,60 @@
         ext[base + 8 * n : base + 8 * n + 8, :] = value
 
 
-def project_slab(chunk, slab, ext, phi_t, tab, part):
+def project_slab(chunk, slab, ext, phi_t, tab, part, accs):
     lane = lane_iota()
     for zz in range(8):
         extend(chunk[zz], ext, zz * EXT)
+
+    def some_views(g, _):
+        offs = tab.at[0, pl.ds(g * GROUP, GROUP), pl.ds(slab * 8, 8)]
+        phis = phi_t.at[pl.ds(g * GROUP, GROUP), pl.ds(slab * 8, 8), :]
+        for j in range(GROUP):
+            acc = None
+            for zz in range(8):
+                off = offs[j, zz]
+                a = ext[pl.ds(off, 8), :]
+                b = ext[pl.ds(off + 1, 8), :]
+                term = a + row_of(phis.at[j], zz) * (b - a)
+                acc = term if acc is None else acc + term
+            accs[g * GROUP + j] = acc
+        return 0
+
+    lax.fori_loop(0, VIEWS // GROUP, some_views, 0)
+    kcs = tab.at[1, :, pl.ds(slab * 8, 8)]
     for v in range(VIEWS):
-        acc = None
-        for zz in range(8):
-            off = tab[0, v, slab * 8 + zz] + zz * EXT
-            a = ext[pl.ds(off, 8), :]
-            b = ext[pl.ds(off + 1, 8), :]
-            phi = row_of(phi_t.at[v], slab * 8 + zz)
-            term = a + phi * (b - a)
-            acc = term if acc is None else acc + term
-        kc = tab[1, v, slab * 8]
+        kc = kcs[v, 0]
         pos = lane + kc
-        moved = pltpu.roll(acc, (L - kc) & (L - 1), 1)
+        moved = pltpu.roll(accs[v], (L - kc) & (L - 1), 1)
         part[v] += jnp.where((pos >= -2) & (pos < L), moved, 0.0)
 
 
 def backproject_slab(slab, bw, ext, phi_t, tab, out):
     lane = lane_iota()
+    kcs = tab.at[3, :, pl.ds(slab * 8, 8)]
     for v in range(VIEWS):
-        kc = tab[3, v, slab * 8]
+        kc = kcs[v, 0]
         row = bw[v]
         for n in range(3):
             pos = lane + (kc + n)
             moved = pltpu.roll(row, (2 * L - kc - n) & (L - 1), 1)
             ext[v * 24 + 8 * n : v * 24 + 8 * n + 8, :] = jnp.where((pos >= 0) & (pos < L), moved, 0.0)
-    for zz in range(8):
-        acc = None
-        for v in range(VIEWS):
-            off = tab[2, v, slab * 8 + zz] + v * 24
-            b = ext[pl.ds(off, 8), :]
-            a = ext[pl.ds(off + 1, 8), :]
-            phi = row_of(phi_t.at[v], slab * 8 + zz)
-            term = a + phi * (b - a)
-            acc = term if acc is None else acc + term
-        out[zz] = acc
+
+    def layers(n, _):
+        offs = tab.at[2, :, pl.ds(slab * 8 + n * AT_ONCE, AT_ONCE)]
+        phis = phi_t.at[:, pl.ds(slab * 8 + n * AT_ONCE, AT_ONCE), :]
+        for zz in range(AT_ONCE):
+            accs = [None] * 4
+            for v in range(VIEWS):
+                off = offs[v, zz]
+                b = ext[pl.ds(off, 8), :]
+                a = ext[pl.ds(off + 1, 8), :]
+                term = a + row_of(phis.at[v], zz) * (b - a)
+                accs[v % 4] = term if v < 4 else accs[v % 4] + term
+            out[n * AT_ONCE + zz] = (accs[0] + accs[1]) + (accs[2] + accs[3])
+        return 0
+
+    lax.fori_loop(0, 8 // AT_ONCE, layers, 0)
 
 
 def to_tiles(read, batch, turned, tiles):
@@ -117,10 +138,10 @@
 
 
 def kernel(
-    volume, angles, det, measured,
+    volume, angles_in, det_in, measured,
     grad_in, res_in,
     vb, mbuf, m16, turned, tiles, xsend, xin, abuf, sf, wt, tab_v, phi_t, ext, ext_b,
-    part, pin, bw, mtiles, mi, mr, m2, msend, m3, rsend, r2, rs2, r3, xres, gsend, tab,
+    part, pin, bw, mtiles, mi, mr, m2, msend, m3, rsend, r2, rs2, r3, xres, gsend, accs, hot, hot_t, det, tab, angles,
     loc_sem, vol_send, vol_recv, ang_send, ang_recv, part_send, part_recv,
     mid_send, mid_recv, grad_send, grad_recv,
 ):
@@ -130,8 +151,10 @@
 
     load_v = pltpu.make_async_copy(volume.at[:, pl.ds(pl.multiple_of(vert * 16, 16), 16), :], vb, loc_sem.at[0])
     load_m = pltpu.make_async_copy(measured, mbuf, loc_sem.at[1])
-    load_v.start()
-    load_m.start()
+    load_a = pltpu.make_async_copy(angles_in, angles, loc_sem.at[3])
+    load_d = pltpu.make_async_copy(det_in, det, loc_sem.at[4])
+    for load in (load_a, load_v, load_m, load_d):
+        load.start()
 
     def greet_gz(i, _):
         pl.semaphore_signal(barrier, inc=1, device_id=at(lax.rem(gz + i, 32), vert))
@@ -145,6 +168,8 @@
     lax.fori_loop(1, VERT, greet_vert, 0)
 
     sub = sub_iota()
+    load_a.wait()
+    load_d.wait()
     slope = jnp.zeros((8, L), jnp.int32)
     for i in range(4):
         slope = jnp.where(sub % 4 == i, jnp.full((8, L), 2 * angles[i] - 512), slope)
@@ -166,6 +191,12 @@
     lax.fori_loop(0, CHIPS, gather_rows, 0)
     for zz in range(8):
         xin[p, zz] = xsend[p, zz]
+
+    @pl.when(core == MID)
+    def _():
+        for bit in range(2):
+            hot[bit] = one_hot(det[...], bit)
+            hot_t[bit] = jnp.transpose(hot[bit])
 
     pl.semaphore_wait(barrier, 31 + 7)
 
@@ -222,10 +253,10 @@
     k_min, k_max = jnp.minimum(*ends), jnp.maximum(*ends)
     k = ((first + lane % 8) * s) >> 9
     kc = jnp.where(k_min < 0, jnp.minimum(k_min >> 3, -2), k_min >> 3)
-    tab_v[0] = k - 8 * kc + jnp.where(k_min < 0, 24, 0)
+    tab_v[0] = k - 8 * kc + jnp.where(k_min < 0, 24, 0) + (lane % 8) * EXT
     tab_v[1] = kc
     kb = (-k_max - 1) >> 3
-    tab_v[2] = -k - 1 - 8 * kb
+    tab_v[2] = -k - 1 - 8 * kb + 24 * lax.broadcasted_iota(jnp.int32, (VIEWS, L), 0)
     tab_v[3] = kb
     to_smem = pltpu.make_async_copy(tab_v, tab, loc_sem.at[2])
     to_smem.start()
@@ -238,6 +269,25 @@
         return 0
 
     lax.fori_loop(0, VIEWS, fill_phi, 0)
+
+    @pl.when(core == MID)
+    def _():
+        pltpu.make_async_copy(mi.at[pl.ds(0, 31)], mi.at[pl.ds(0, 31)], mid_recv.at[0]).wait()
+        got = mi[...].reshape(2 * L, L)
+        for bit in range(2):
+            rows = jnp.dot(hot[bit], got, precision=HIGH, preferred_element_type=F32)
+            mr[:, bit] = rows.reshape(VERT, 16, L)
+
+        def send(n, _):
+            w = lax.rem(vert + n, VERT)
+            pltpu.make_async_remote_copy(
+                mr.at[w], m2.at[vert], mid_send.at[1], mid_recv.at[1], device_id=at(gz, w)
+            ).start()
+            return 0
+
+        lax.fori_loop(1, VERT, send, 0)
+        m2[vert] = mr[vert]
+
     to_smem.wait()
 
     def project_step(i, _):
@@ -247,27 +297,9 @@
         def _():
             pltpu.make_async_copy(xin.at[q], xin.at[q], vol_recv.at[q]).wait()
 
-        project_slab(xin.at[q], q, ext, phi_t, tab, part)
-
-        @pl.when((core == MID) & (i == 3))
-        def _():
-            pltpu.make_async_copy(mi.at[pl.ds(0, 31)], mi.at[pl.ds(0, 31)], mid_recv.at[0]).wait()
-            got = mi[...].reshape(2 * L, L)
-            for bit in range(2):
-                rows = jnp.dot(one_hot(det[...], bit), got, precision=HIGH, preferred_element_type=F32)
-                mr[:, bit] = rows.reshape(VERT, 16, L)
-
-            def send(n, _):
-                w = lax.rem(vert + n, VERT)
-                pltpu.make_async_remote_copy(
-                    mr.at[w], m2.at[vert], mid_send.at[1], mid_recv.at[1], device_id=at(gz, w)
-                ).start()
-                return 0
-
-            lax.fori_loop(1, VERT, send, 0)
-            m2[vert] = mr[vert]
-
-        @pl.when((core == MID) & (i == 7))
+        project_slab(xin.at[q], q, ext, phi_t, tab, part, accs)
+
+        @pl.when((core == MID) & (i == FORWARD_AT))
         def _():
             pltpu.make_async_copy(m2.at[pl.ds(0, 7)], m2.at[pl.ds(0, 7)], mid_recv.at[1]).wait()
             flat = m2.reshape(256, L)
@@ -343,7 +375,7 @@
         def _():
             grad_copy(q).start()
 
-        @pl.when((core == MID) & (i == 3))
+        @pl.when((core == MID) & (i == BACK_AT))
         def _():
             @pl.when(own_mid)
             def _():
@@ -368,30 +400,31 @@
             lax.fori_loop(1, VERT, send, 0)
             r3[vert] = rs2[vert]
 
-        @pl.when((core == MID) & (i == 7))
-        def _():
-            pltpu.make_async_copy(r3.at[pl.ds(0, 7)], r3.at[pl.ds(0, 7)], mid_recv.at[4]).wait()
-            total = None
-            for bit in range(2):
-                rows = r3[:, bit].reshape(L, L)
-                hot = jnp.transpose(one_hot(det[...], bit))
-                out = jnp.dot(hot, rows, precision=HIGH, preferred_element_type=F32)
-                total = out if total is None else total + out
-            xres[...] = total.reshape(32, 8, L)
-
-            def send(n, _):
-                w = lax.rem(gz + n, 32)
-                pltpu.make_async_remote_copy(
-                    xres.at[w], res_in.at[p], mid_send.at[5], mid_recv.at[5], device_id=at(w, vert)
-                ).start()
-                return 0
-
-            lax.fori_loop(1, 32, send, 0)
-            pltpu.make_async_copy(xres.at[gz], res_in.at[p], loc_sem.at[3]).start()
-
         return 0
 
     lax.fori_loop(0, CHIPS, back_step, 0)
+
+    @pl.when(core == MID)
+    def _():
+        pltpu.make_async_copy(r3.at[pl.ds(0, 7)], r3.at[pl.ds(0, 7)], mid_recv.at[4]).wait()
+        total = None
+        for bit in range(2):
+            rows = r3[:, bit].reshape(L, L)
+
+            out = jnp.dot(hot_t[bit], rows, precision=HIGH, preferred_element_type=F32)
+            total = out if total is None else total + out
+        xres[...] = total.reshape(32, 8, L)
+
+        def send(n, _):
+            w = lax.rem(gz + n, 32)
+            pltpu.make_async_remote_copy(
+                xres.at[w], res_in.at[p], mid_send.at[5], mid_recv.at[5], device_id=at(w, vert)
+            ).start()
+            return 0
+
+        lax.fori_loop(1, 32, send, 0)
+        pltpu.make_async_copy(xres.at[gz], res_in.at[p], loc_sem.at[3]).start()
+
     own_grad = pltpu.make_async_copy(gsend.at[p], grad_in.at[p], loc_sem.at[4])
     own_grad.start()
 
@@ -428,7 +461,7 @@
 
 def exchange(volume, angles, det, measured):
     dma = pltpu.SemaphoreType.DMA
-    any_space = pl.BlockSpec(memory_space=pl.ANY)
+    hbm = pl.BlockSpec(memory_space=pltpu.HBM)
     vmem = lambda *dims, dtype=F32: pltpu.VMEM(dims, dtype)
     scratch = [
         vmem(8, 16, 1024), vmem(4, 4, 1024), vmem(16, 1024), vmem(1024, L), vmem(1024, L),
@@ -437,26 +470,26 @@
         vmem(VIEWS, 8, L), vmem(VIEWS, 8, L), vmem(VIEWS, 8, L), vmem(L, L), vmem(32, 8, L), vmem(VERT, 2, 16, L),
         vmem(VERT, 2, 16, L), vmem(CHIPS, 16, L), vmem(CHIPS, 16, L), vmem(8, 16, L), vmem(CHIPS, 16, L),
         vmem(VERT, 2, 16, L), vmem(VERT, 2, 16, L), vmem(32, 8, L), vmem(CHIPS, 8, 8, L),
-        pltpu.SMEM((4, VIEWS, L), jnp.int32),
+        vmem(VIEWS, 8, L), vmem(2, L, 2 * L), vmem(2, 2 * L, L), vmem(1, L, dtype=jnp.int32), pltpu.SMEM((4, VIEWS, L), jnp.int32), pltpu.SMEM((4,), jnp.int32),
         dma((5,)), dma, dma((CHIPS,)), dma, dma, dma, dma, dma((6,)), dma((6,)), dma, dma,
     ]
     return pl.pallas_call(
         kernel,
         out_shape=[jax.ShapeDtypeStruct((CHIPS, 8, 8, L), F32), jax.ShapeDtypeStruct((CHIPS, 8, L), F32)],
-        in_specs=[
-            any_space,
-            pl.BlockSpec(memory_space=pltpu.SMEM),
-            pl.BlockSpec(memory_space=pltpu.VMEM),
-            any_space,
-        ],
-        out_specs=[any_space, any_space],
+        in_specs=[hbm, hbm, hbm, hbm],
+        out_specs=[hbm, hbm],
         scratch_shapes=scratch,
-        compiler_params=pltpu.CompilerParams(collective_id=0, has_side_effects=True, vmem_limit_bytes=40 * 2**20),
+        compiler_params=pltpu.CompilerParams(collective_id=0, has_side_effects=True, vmem_limit_bytes=ALL_VMEM),
         name="exchange",
     )(volume, angles, det, measured)
 
 
-def finish_kernel(grad_in, res_in, res_out, grad_out, turned):
+def finish_kernel(grad_hbm, res_hbm, res_hbm_out, grad_hbm_out, grad_in, res_in, res_out, grad_out, turned, sem):
+    load_r = pltpu.make_async_copy(res_hbm, res_in, sem.at[0])
+    load_g = pltpu.make_async_copy(grad_hbm, grad_in, sem.at[1])
+    load_r.start()
+    load_g.start()
+    load_r.wait()
     for r in range(8):
         both = jnp.concatenate([res_in[r], res_in[8 + r]], axis=0)
         turned[pl.ds(r, L, stride=8), 0:16] = jnp.transpose(both)
@@ -464,21 +497,33 @@
         rows = jnp.transpose(turned[t * L : (t + 1) * L, 0:16])
         for a in range(4):
             res_out[a, :, t * L : (t + 1) * L] = rows[4 * a : 4 * a + 4]
+    store_r = pltpu.make_async_copy(res_out, res_hbm_out, sem.at[2])
+    store_r.start()
+    load_g.wait()
     flat = grad_in.reshape(CHIPS * 64, L)
     for r in range(8):
         rows = [flat[pl.ds(zz * 8 + r, 16, stride=64), :] for zz in range(8)]
         turned[pl.ds(r, L, stride=8), :] = jnp.transpose(jnp.concatenate(rows, axis=0))
     for t in range(8):
         grad_out[:, :, t * L : (t + 1) * L] = jnp.transpose(turned[t * L : (t + 1) * L, :]).reshape(8, 16, L)
+    store_g = pltpu.make_async_copy(grad_out, grad_hbm_out, sem.at[3])
+    store_g.start()
+    store_r.wait()
+    store_g.wait()
 
 
 def finish(grad_in, res_in):
+    hbm = pl.BlockSpec(memory_space=pltpu.HBM)
     return pl.pallas_call(
         finish_kernel,
         out_shape=[jax.ShapeDtypeStruct((4, 4, 1024), F32), jax.ShapeDtypeStruct((8, 16, 1024), F32)],
-        in_specs=[pl.BlockSpec(memory_space=pltpu.VMEM)] * 2,
-        out_specs=[pl.BlockSpec(memory_space=pltpu.VMEM)] * 2,
-        scratch_shapes=[pltpu.VMEM((1024, L), F32)],
+        in_specs=[hbm, hbm],
+        out_specs=[hbm, hbm],
+        scratch_shapes=[
+            pltpu.VMEM((CHIPS, 8, 8, L), F32), pltpu.VMEM((CHIPS, 8, L), F32), pltpu.VMEM((4, 4, 1024), F32),
+            pltpu.VMEM((8, 16, 1024), F32), pltpu.VMEM((1024, L), F32), pltpu.SemaphoreType.DMA((4,)),
+        ],
+        compiler_params=pltpu.CompilerParams(vmem_limit_bytes=ALL_VMEM),
         name="finish",
     )(grad_in, res_in)
 

time: 63.2 us -> 55.3 us (0.87)
  local copies, waits for them, and re-layouts: 5.74 us -> 0 us
  Pallas kernels: 56.1 us -> 54 us
    unnamed x12 -> x0, local copies, waits for them, and re-layouts: 5.74 us -> none
    pallas_call x1, Pallas kernels: 53.4 us -> 51.4 us  [exchange(): pl.pallas_call(kernel, out_shape=[jax.ShapeDtypeStruct((CHIPS, 8, 8, L),...]
where the time goes in v2:
time: 55.3 us; the launch traced here: 54.6 us
  Pallas kernels  54 us (98%)
  between operations  0.64 us (1%)
    pallas_call x1, Pallas kernels, exchange(): pl.pallas_call(kernel, out_shape=[jax.ShapeDtypeStruct((CHIPS, 8, 8, L),...  51.4 us
    pallas_call x1, Pallas kernels, finish(): pl.pallas_call(finish_kernel, out_shape=[jax.ShapeDtypeStruct((4, 4, 1024...  2.6 us

profile of v2, /device:TPU:1, one launch (start us, length us, event | category | flops | bytes accessed | tf_op | source)
XLA Modules:
  0.0 54.6 jit_solution(11595119593178875358)
XLA Ops:
  0.6 51.4 %exchange.1 = (f32[16,8,8,128]{3,2,1,0:T(8,128)}, f32[16,8,128]{2,1,0:T(8,128)}) custom-call(f32[8,128,1024]{2,1,0:T(8,128)} %volume.1, s32[4]{0:T(128)} %angles_in.1, s32[1,128]{1,0:T(1,128)} %bitcast.1, f32[4,4,1024]{2,1,0:T(4,128)} %measured.1), custom_call_target="tpu_custom_call" | custom-call | tf_op jit(solution)/shard_map/exchange/pallas_call | solution.py:476
  52.0 2.6 %finish.1 = (f32[4,4,1024]{2,1,0:T(4,128)}, f32[8,16,1024]{2,1,0:T(8,128)}) custom-call(f32[16,8,8,128]{3,2,1,0:T(8,128)} %get-tuple-element.4.grad_hbm, f32[16,8,128]{2,1,0:T(8,128)} %get-tuple-element.5.res_hbm), custom_call_target="tpu_custom_call" | custom-call | tf_op jit(solution)/shard_map/finish/pallas_call | solution.py:517

commit v3 on v2

--- a/solution.py
+++ b/solution.py
@@ -33,11 +33,16 @@
 
 
 def visit(i, p):
-    step = lax.div(i, 2)
+    step = lax.rem(i, 8)
     far = lax.div(step + 1, 2)
     dz = jnp.where(lax.rem(step, 2) == 1, far, 8 - far)
     z = lax.rem(lax.div(p, 2) + dz, 8)
-    return z * 2 + lax.rem(p + i, 2)
+    return z * 2 + lax.rem(p + lax.div(i, 8), 2)
+
+
+def mixed(i):
+    half = lax.div(i, 2)
+    return jnp.where(i == CHIPS - 1, 0, jnp.where(lax.rem(i, 2) == 0, 1 + half, CHIPS - 1 - half))
 
 
 def row_of(ref, r):
@@ -368,7 +373,7 @@
         )
 
     def back_step(i, _):
-        q = visit(CHIPS - 1 - i, p)
+        q = visit(mixed(i), p)
         backproject_slab(q, bw, ext_b, phi_t, tab, gsend.at[q])
 
         @pl.when(i < CHIPS - 1)

time: 55.3 us -> 54 us (0.976); the launches traced: 54.6 us -> 53.9 us
  Pallas kernels: 54 us -> 53.3 us
    pallas_call x1, Pallas kernels: 51.4 us -> 50.7 us  [exchange(): pl.pallas_call(kernel, out_shape=[jax.ShapeDtypeStruct((CHIPS, 8, 8, L),...]
where the time goes in v3:
time: 54 us; the launch traced here: 53.9 us
  Pallas kernels  53.3 us (99%)
  between operations  0.64 us (1%)
    pallas_call x1, Pallas kernels, exchange(): pl.pallas_call(kernel, out_shape=[jax.ShapeDtypeStruct((CHIPS, 8, 8, L),...  50.7 us
    pallas_call x1, Pallas kernels, finish(): pl.pallas_call(finish_kernel, out_shape=[jax.ShapeDtypeStruct((4, 4, 1024...  2.6 us

profile of v3, /device:TPU:1, one launch (start us, length us, event | category | flops | bytes accessed | tf_op | source)
XLA Modules:
  0.0 53.9 jit_solution(1889257538220459802)
XLA Ops:
  0.6 50.7 %exchange.1 = (f32[16,8,8,128]{3,2,1,0:T(8,128)}, f32[16,8,128]{2,1,0:T(8,128)}) custom-call(f32[8,128,1024]{2,1,0:T(8,128)} %volume.1, s32[4]{0:T(128)} %angles_in.1, s32[1,128]{1,0:T(1,128)} %bitcast.1, f32[4,4,1024]{2,1,0:T(4,128)} %measured.1), custom_call_target="tpu_custom_call" | custom-call | tf_op jit(solution)/shard_map/exchange/pallas_call | solution.py:481
  51.3 2.6 %finish.1 = (f32[4,4,1024]{2,1,0:T(4,128)}, f32[8,16,1024]{2,1,0:T(8,128)}) custom-call(f32[16,8,8,128]{3,2,1,0:T(8,128)} %get-tuple-element.4.grad_hbm, f32[16,8,128]{2,1,0:T(8,128)} %get-tuple-element.5.res_hbm), custom_call_target="tpu_custom_call" | custom-call | tf_op jit(solution)/shard_map/finish/pallas_call | solution.py:522

commit v4 on v3

--- a/solution.py
+++ b/solution.py
@@ -9,9 +9,9 @@
 CHIPS = 16
 VERT = 8
 VIEWS = 32
-GROUP = 8
-AT_ONCE = 2
-FORWARD_AT = 6
+GROUP = 16
+AT_ONCE = 4
+FORWARD_AT = 8
 BACK_AT = 9
 MID = 1
 EXT = 56

time: 54 us -> 54 us (level)
  no operation moved by 1% of the time
where the time goes in v4:
time: 54 us; the launch traced here: 53.9 us
  Pallas kernels  53.3 us (99%)
  between operations  0.64 us (1%)
    pallas_call x1, Pallas kernels, exchange(): pl.pallas_call(kernel, out_shape=[jax.ShapeDtypeStruct((CHIPS, 8, 8, L),...  50.7 us
    pallas_call x1, Pallas kernels, finish(): pl.pallas_call(finish_kernel, out_shape=[jax.ShapeDtypeStruct((4, 4, 1024...  2.6 us

profile of v4, /device:TPU:1, one launch (start us, length us, event | category | flops | bytes accessed | tf_op | source)
XLA Modules:
  0.0 53.9 jit_solution(1685525930465235622)
XLA Ops:
  0.6 50.7 %exchange.1 = (f32[16,8,8,128]{3,2,1,0:T(8,128)}, f32[16,8,128]{2,1,0:T(8,128)}) custom-call(f32[8,128,1024]{2,1,0:T(8,128)} %volume.1, s32[4]{0:T(128)} %angles_in.1, s32[1,128]{1,0:T(1,128)} %bitcast.1, f32[4,4,1024]{2,1,0:T(4,128)} %measured.1), custom_call_target="tpu_custom_call" | custom-call | tf_op jit(solution)/shard_map/exchange/pallas_call | solution.py:481
  51.3 2.6 %finish.1 = (f32[4,4,1024]{2,1,0:T(4,128)}, f32[8,16,1024]{2,1,0:T(8,128)}) custom-call(f32[16,8,8,128]{3,2,1,0:T(8,128)} %get-tuple-element.4.grad_hbm, f32[16,8,128]{2,1,0:T(8,128)} %get-tuple-element.5.res_hbm), custom_call_target="tpu_custom_call" | custom-call | tf_op jit(solution)/shard_map/finish/pallas_call | solution.py:522
